TPU v7x, 128 devices: a whole 4x4x4 slice. The times are simulated.
128 devices in a mesh: sector: 64 (over x, y, z_lo, core), dof: 2 (over z_hi).
Axes of the slice: x: 4, y: 4, z: 4 (z_hi: 2, z_lo: 2; z = z_hi * 2 + z_lo), core: 2. Of those that a mesh axis runs over, the one named last changes fastest.
Arguments:
- loads: bfloat16 [64, 128, 32768], P('sector', None, 'dof'), may hold values from -0.75 to 0.75
- modes: bfloat16 [32768, 512], P('dof'), may hold values from -0.25 to 0.25
- response: float32 [64, 128, 512], P('sector', None, 'dof'), may hold values from -6 to 6
- pattern: int32 [64], P('sector'), may hold values from 0 to 7
- deviation: float32 [8, 512], replicated, may hold values from -1 to 1
- eigen: float32 [64, 512], replicated, may hold values from 1 to 10
- loss: float32 [512], replicated, may hold values from 0.2 to 0.6
- omega_sq: float32 [64], replicated, may hold values from 0.5 to 12
- iface_left: int32 [1024], P('dof'), may hold values from 0 to 16383, as said below
- iface_right: int32 [1024], P('dof'), may hold values from 0 to 16383, as said below
Outputs:
- modal_response: float32 [64, 128, 512], P('sector', None, 'dof')
- displacement: bfloat16 [64, 128, 32768], P('sector', None, 'dof')
Inputs may be any that keep to these rules, and one draw needn't show every extreme that they name: Within each block of 512 entries, the entries of iface_left and of iface_right together are (2) * 512 distinct rows. `iface_right`: see iface_left.
All inputs are finite; a program needn't handle non-finite values.
Results may differ from a plain program's by a relative error of at most 0.005.
Values may be sent and summed in bfloat16 or wider, within the bound.
No kernel may reach another device: no remote copies, remote signals or barrier semaphores. Data moves between devices by JAX's collectives and lax.ppermute only.
A program may use at most 128 MiB of HBM per device.

v0:
```python
import math

import jax
import jax.numpy as jnp
from jax import lax
from jax.sharding import Mesh
from jax.sharding import PartitionSpec as P

SECTOR = ("sector_0", "sector_1", "sector_2", "sector_3")


def split_up(shard, dim, size):
    dims = shard.shape
    pieces = shard.reshape(*dims[:dim], size, dims[dim] // size, *dims[dim + 1 :])
    return jnp.moveaxis(pieces, dim, 0)


def sent_and_summed(shard, axis, dim):
    size = lax.axis_size(axis)
    pieces = lax.all_to_all(split_up(shard, dim, size), axis, 0, 0, tiled=True)
    return jnp.sum(pieces, axis=0)


def in_order(pieces, dim):
    pieces = jnp.moveaxis(pieces, 0, dim)
    dims = pieces.shape
    return pieces.reshape(*dims[:dim], dims[dim] * dims[dim + 1], *dims[dim + 2 :])


def exchange_in_order(pieces, axes, sequence):
    inside = pieces.shape[1:]
    result = pieces.reshape(*(lax.axis_size(a) for a in axes), *inside)
    for k in sequence:
        result = lax.all_to_all(result, axes[k], k, k, tiled=True)
    return result.reshape(-1, *inside)


def two_step_exchange(shard, groups, sequence, split_dim, concat_dim):
    size = lax.axis_size(groups[0]) * lax.axis_size(groups[1])
    pieces = split_up(shard, split_dim, size)
    return in_order(exchange_in_order(pieces, groups, sequence), concat_dim)


def copy_for_each(shard, axis):
    size = lax.axis_size(axis)
    return lax.all_to_all(
        jnp.broadcast_to(shard[None], (size, *shard.shape)), axis, 0, 0, tiled=True
    )


def gather_directly(shard, axis, dim):
    pieces = copy_for_each(shard, axis)
    return in_order(pieces, dim)


def shifted_2(shard, axis, by):
    size = lax.axis_size(axis)
    return lax.ppermute(shard, axis, [(i, (i + by) % size) for i in range(size)])


def tables(row_count, col_count, sectors):
    rows_idx = jnp.arange(row_count, dtype=jnp.int32) % sectors
    cols_idx = jnp.arange(col_count, dtype=jnp.int32) % sectors
    turns = rows_idx[:, None] * cols_idx[None, :] % sectors
    theta = turns.astype(jnp.float32) * (2.0 * math.pi / sectors)
    return (jnp.cos(theta), jnp.sin(theta))


def divide(spec_re, spec_im, shifted, damped):
    denom = shifted * shifted + damped * damped
    return (
        (spec_re * shifted + spec_im * damped) / denom,
        (spec_im * shifted - spec_re * damped) / denom,
    )


def shards(
    loads, modes, response, pattern, deviation, eigen, loss, omega_sq, iface_left, iface_right
):
    highest = lax.Precision.HIGHEST
    local_sec, rows_two, dof_rows = loads.shape
    freqs = rows_two // 2
    modes_all = modes.shape[1]
    sec_devices = lax.axis_size(SECTOR)
    sectors = sec_devices * local_sec
    half = modes_all // lax.axis_size("dof")
    width = freqs * half
    first_mode = lax.axis_index("dof") * half
    partial_force = jnp.dot(
        loads.reshape(local_sec * rows_two, dof_rows), modes, preferred_element_type=jnp.float32
    )
    force = sent_and_summed(partial_force.reshape(local_sec, rows_two, modes_all), "dof", 2)
    table_count = deviation.shape[0]
    dev_half = lax.dynamic_slice_in_dim(deviation, first_mode, half, 1)
    onehot = (pattern[:, None] == jnp.arange(table_count, dtype=jnp.int32)[None, :]).astype(
        jnp.float32
    )
    dev_rows = jnp.dot(onehot, dev_half, precision=highest)
    rest = (force - dev_rows[:, None, :] * response).reshape(local_sec, 2, width)
    columns = two_step_exchange(
        rest, (("sector_0", "sector_1", "sector_2"), "sector_3"), (1, 0), 2, 0
    )
    share = width // sec_devices
    col_idx = lax.axis_index(SECTOR) * share + jnp.arange(share, dtype=jnp.int32)
    freq_idx = col_idx // half
    mode_idx = first_mode + col_idx % half
    stiff = jnp.take(eigen, mode_idx, axis=1)
    shifted = stiff - jnp.take(omega_sq, freq_idx)[None, :]
    damped = jnp.take(loss, mode_idx)[None, :] * stiff
    cosine, sine = tables(sectors, sectors, sectors)
    spec_re = jnp.dot(cosine, columns[:, 0], precision=highest) + jnp.dot(
        sine, columns[:, 1], precision=highest
    )
    spec_im = jnp.dot(cosine, columns[:, 1], precision=highest) - jnp.dot(
        sine, columns[:, 0], precision=highest
    )
    solved_re, solved_im = divide(spec_re, spec_im, shifted, damped)
    out_re = (
        jnp.dot(cosine, solved_re, precision=highest) - jnp.dot(sine, solved_im, precision=highest)
    ) / sectors
    out_im = (
        jnp.dot(cosine, solved_im, precision=highest) + jnp.dot(sine, solved_re, precision=highest)
    ) / sectors
    updated = lax.all_to_all(
        jnp.stack([out_re, out_im], 1).astype(jnp.bfloat16),
        SECTOR,
        split_axis=0,
        concat_axis=2,
        tiled=True,
    ).astype(jnp.float32)
    modal_response = updated.reshape(local_sec, rows_two, half)
    rounded = modal_response.astype(jnp.bfloat16)
    raw = jnp.einsum(
        "skm,dm->skd", gather_directly(rounded, "dof", 2), modes, preferred_element_type=jnp.float32
    ).astype(jnp.bfloat16)
    left_vals = jnp.take(raw, iface_left, axis=2)
    right_vals = jnp.take(raw, iface_right, axis=2)
    next_left = shifted_2(left_vals, SECTOR, -1)
    prev_right = shifted_2(right_vals, SECTOR, 1)
    left_after = jnp.concatenate([left_vals[1:], next_left], 0)
    right_before = jnp.concatenate([prev_right, right_vals[:-1]], 0)
    right_new = (0.5 * (right_vals.astype(jnp.float32) + left_after.astype(jnp.float32))).astype(
        jnp.bfloat16
    )
    left_new = (0.5 * (right_before.astype(jnp.float32) + left_vals.astype(jnp.float32))).astype(
        jnp.bfloat16
    )
    displacement = raw.at[:, :, iface_right].set(right_new).at[:, :, iface_left].set(left_new)
    return (modal_response, displacement)


def solution(mesh):
    torus = Mesh(
        mesh.devices.reshape(4, 4, 2, 2, mesh.shape["dof"]),
        ("sector_0", "sector_1", "sector_2", "sector_3", "dof"),
    )
    return jax.shard_map(
        shards,
        mesh=torus,
        in_specs=(
            P(SECTOR, None, "dof"),
            P("dof", None),
            P(SECTOR, None, "dof"),
            P(SECTOR),
            P(),
            P(),
            P(),
            P(),
            P("dof"),
            P("dof"),
        ),
        out_specs=(P(SECTOR, None, "dof"), P(SECTOR, None, "dof")),
        check_vma=False,
    )
```

profile of v0, /device:TPU:1, one launch (start us, length us, event | category | flops | bytes accessed | tf_op | source)
XLA Modules:
  0.0 142.7 jit_solution(1476875651069845585)
XLA Ops:
  0.6 21.3 %copy.54 = bf16[512,16384]{1,0:T(8,128)(2,1)} copy(bf16[512,16384]{0,1:T(8,128)(2,1)} %bitcast.125) | data formatting | bytes 33554432 | tf_op jit(solution)/shard_map/dot_general | solution.py:89
  22.0 13.5 %fusion.2 = f32[2,1,128,256]{3,2,1,0:T(8,128)} fusion(bf16[2,256,16384]{2,1,0:T(8,128)(2,1)} %bitcast.124, bf16[1,128,16384]{2,1,0:T(8,128)(2,1)} %param.12), kind=kOutput, calls=%fused_computation.10 | convolution fusion | flops 2147483648 | bytes 21233664 | tf_op jit(solution)/shard_map/dot_general | solution.py:89
  35.5 5.8 %all-to-all-start = ((f32[2,1,128,256]{3,2,1,0:T(8,128)}), f32[2,1,128,256]{3,2,1,0:T(8,128)S(1)}, u32[]{:S(2)}, u32[]{:S(2)}) async-start(f32[2,1,128,256]{3,2,1,0:T(8,128)} %fusion.2), calls=%async_computation | async-start | bytes 524288 | tf_op jit(solution)/shard_map/all_to_all | solution.py:20
  41.4 1.9 %gather_fusion.2 = f32[256]{0:T(256)S(1)} fusion(f32[512]{0:T(512)S(1)} %copy-done.2, s32[1024]{0:T(1024)S(1)} %pad_clamp_fusion.3), kind=kCustom, calls=%fused_computation.4 | custom fusion | bytes 3072 | tf_op jit(solution)/shard_map/jit(_take)/gather | solution.py:109
  44.0 1.9 %gather_fusion.1 = f32[256]{0:T(256)S(1)} fusion(f32[64]{0:T(128)S(1)} %copy-done.1, s32[1024]{0:T(1024)S(1)} %pad_clamp_fusion.2), kind=kCustom, calls=%fused_computation.3 | custom fusion | bytes 3072 | tf_op jit(solution)/shard_map/jit(_take)/gather | solution.py:108
  46.0 0.8 all-to-all-done
  47.0 5.6 %all_to_all.35 = f32[32,2,1,2,256]{4,0,3,2,1:T(8,128)S(1)} all-to-all(f32[32,2,1,2,256]{4,0,3,2,1:T(8,128)S(1)} %copy.41), channel_id=1, replica_groups=mesh['sector_0'=4,'sector_1'=4,'sector_2'=2,'sector_3'=2,'dof'=2] {'sect..., dimensions={1} | all-to-all | bytes 262144 | tf_op jit(solution)/shard_map/all_to_all | solution.py:34
  52.6 0.8 copy.42
  53.4 7.5 %all-to-all-start.2 = ((f32[32,2,1,2,256]{4,1,3,2,0:T(2,128)}), f32[32,2,1,2,256]{4,1,3,2,0:T(2,128)S(1)}, u32[]{:S(2)}, u32[]{:S(2)}) async-start(f32[32,2,1,2,256]{4,1,3,2,0:T(2,128)} %copy.42), calls=%async_computation.2 | async-start | bytes 262144 | tf_op jit(solution)/shard_map/all_to_all | solution.py:34
  61.0 0.7 gather_fusion
  61.8 6.3 %all-to-all-done.2 = f32[32,2,1,2,256]{4,1,3,2,0:T(2,128)S(1)} async-done(((f32[32,2,1,2,256]{4,1,3,2,0:T(2,128)}), f32[32,2,1,2,256]{4,1,3,2,0:T(2,128)S(1)}, u32[]{:S(2)}, u32[]{:S(2)}) %all-to-all-start.2) | async-done | bytes 131104 | tf_op jit(solution)/shard_map/all_to_all | solution.py:34
  71.5 0.7 copy.46
  72.2 5.9 %all-to-all-start.3 = ((bf16[64,2,256]{2,1,0:T(2,128)(2,1)}), bf16[64,2,256]{2,1,0:T(2,128)(2,1)S(1)}, u32[]{:S(2)}, u32[]{:S(2)}) async-start(bf16[64,2,256]{2,1,0:T(2,128)(2,1)} %copy.46), calls=%async_computation.3 | async-start | bytes 131072 | tf_op jit(solution)/shard_map/all_to_all | solution.py:124
  78.1 8.1 %all-to-all-done.3 = bf16[64,2,256]{2,1,0:T(2,128)(2,1)S(1)} async-done(((bf16[64,2,256]{2,1,0:T(2,128)(2,1)}), bf16[64,2,256]{2,1,0:T(2,128)(2,1)S(1)}, u32[]{:S(2)}, u32[]{:S(2)}) %all-to-all-start.3) | async-done | bytes 65568 | tf_op jit(solution)/shard_map/all_to_all | solution.py:124
  87.1 3.6 %all-to-all-start.4 = ((bf16[2,1,128,256]{2,3,1,0:T(8,128)(2,1)}), bf16[2,1,128,256]{2,3,1,0:T(8,128)(2,1)S(1)}, u32[]{:S(2)}, u32[]{:S(2)}) async-start(bf16[2,1,128,256]{2,3,1,0:T(8,128)(2,1)} %broadcast_in_dim.54), calls=%async_computation.4 | async-start | bytes 262144 | tf_op jit(solution)/shard_map/all_to_all | solution.py:46
  90.7 4.6 %all-to-all-done.4 = bf16[2,1,128,256]{2,3,1,0:T(8,128)(2,1)S(1)} async-done(((bf16[2,1,128,256]{2,3,1,0:T(8,128)(2,1)}), bf16[2,1,128,256]{2,3,1,0:T(8,128)(2,1)S(1)}, u32[]{:S(2)}, u32[]{:S(2)}) %all-to-all-start.4) | async-done | bytes 131104 | tf_op jit(solution)/shard_map/all_to_all | solution.py:46
  95.3 10.4 %convolution_convert_fusion = bf16[128,16384]{1,0:T(8,128)(2,1)} fusion(bf16[128,512]{0,1:T(8,128)(2,1)S(1)} %bitcast.128, bf16[16384,512]{1,0:T(8,128)(2,1)} %param.13), kind=kOutput, calls=%fused_computation.7 | convolution fusion | flops 2149580800 | bytes 21102592 | tf_op jit(solution)/shard_map/skm,dm->skd/dot_general | solution.py:133
  105.7 6.4 %copy.52 = bf16[128,16384]{0,1:T(8,128)(2,1)} copy(bf16[128,16384]{1,0:T(8,128)(2,1)} %convolution_convert_fusion) | data formatting | bytes 8388608 | tf_op jit(solution)/shard_map/convert_element_type | solution.py:135
  112.1 3.8 %gather_fusion.4 = bf16[512,128]{1,0:T(8,128)(2,1)S(1)} fusion(bf16[128,16384]{0,1:T(8,128)(2,1)} %copy.52, s32[1024]{0:T(1024)S(1)} %pad_clamp_fusion), kind=kCustom, calls=%fused_computation.1.clone | custom fusion | bytes 264192 | tf_op jit(solution)/shard_map/jit(_take)/gather | solution.py:136
  116.0 1.8 %collective-permute-start = (bf16[1,128,512]{1,2,0:T(8,128)(2,1)S(1)}, bf16[1,128,512]{1,2,0:T(8,128)(2,1)S(1)}, u32[]{:S(2)}, u32[]{:S(2)}) collective-permute-start(bf16[1,128,512]{1,2,0:T(8,128)(2,1)S(1)} %bitcast_select_fusion), channel_id=1, source_target_pairs={{0,126},{2,0},{4,2},{6,4},{8,6},{10,8},{12,10},{14,12},{16,14},{18... | collective-permute-start | bytes 393224 | tf_op jit(solution)/shard_map/ppermute | solution.py:58
  117.8 3.8 %gather_fusion.3 = bf16[512,128]{1,0:T(8,128)(2,1)S(1)} fusion(bf16[128,16384]{0,1:T(8,128)(2,1)} %copy.52, s32[1024]{0:T(1024)S(1)} %pad_clamp_fusion.1), kind=kCustom, calls=%fused_computation.clone | custom fusion | bytes 264192 | tf_op jit(solution)/shard_map/jit(_take)/gather | solution.py:137
  122.6 6.9 %scatter_custom_fusion = bf16[128,16384]{0,1:T(8,128)(2,1)} fusion(bf16[128,16384]{0,1:T(8,128)(2,1)} %copy.52, s32[512]{0:T(512)S(1)} %compare_select_fusion.3, bf16[1,128,512]{1,2,0:T(8,128)(2,1)S(1)} %collective-permute-done, f32[]{:T(128)} %constant.148.clone.1, bf16[512,128]{1,0:T(8,128)(2,1)S(1)} %gather_fusion.3, pred[512]{0:T(512)(128)(4,1)S(1)} %compare_and_fusion.1), kind=kCustom, calls=%fused_computation.24 | custom fusion | flops 393216 | bytes 4457472 | tf_op jit(solution)/shard_map/scatter | solution.py:148
  129.4 6.9 %scatter_custom_fusion.1 = bf16[128,16384]{0,1:T(8,128)(2,1)} fusion(bf16[128,16384]{0,1:T(8,128)(2,1)} %scatter_custom_fusion, s32[512]{0:T(512)S(1)} %compare_select_fusion.2, bf16[1,128,512]{1,2,0:T(8,128)(2,1)S(1)} %collective-permute-done.1, f32[]{:T(128)} %constant.148.clone.1, bf16[512,128]{1,0:T(8,128)(2,1)S(1)} %gather_fusion.4, ...), kind=kCustom, calls=%fused_computation.26 | custom fusion | flops 393216 | bytes 4457472 | tf_op jit(solution)/shard_map/scatter | solution.py:148
  136.3 6.4 %copy.53 = bf16[1,128,16384]{2,1,0:T(8,128)(2,1)} copy(bf16[1,128,16384]{1,2,0:T(8,128)(2,1)} %bitcast.126) | data formatting | bytes 8388608
  (53 shorter events, 5.8 us)
Async XLA Ops:
  0.6 45.3 %copy-start = (f32[8,512]{1,0:T(8,128)S(1)}, f32[8,512]{1,0:T(8,128)}, u32[]{:S(2)}) copy-start(f32[8,512]{1,0:T(8,128)} %param.16) | copy-start | bytes 49156
  21.9 19.3 %copy-start.5 = (s32[512]{0:T(512)S(1)}, s32[512]{0:T(512)}, u32[]{:S(2)}) copy-start(s32[512]{0:T(512)} %param.20) | copy-start | bytes 6148
  21.9 19.3 %copy-start.6 = (s32[512]{0:T(512)S(1)}, s32[512]{0:T(512)}, u32[]{:S(2)}) copy-start(s32[512]{0:T(512)} %param.21) | copy-start | bytes 6148
  21.9 19.4 %copy-start.2 = (f32[512]{0:T(512)S(1)}, f32[512]{0:T(512)}, u32[]{:S(2)}) copy-start(f32[512]{0:T(512)} %param.18) | copy-start | bytes 6148
  21.9 22.1 %copy-start.1 = (f32[64]{0:T(128)S(1)}, f32[64]{0:T(128)}, u32[]{:S(2)}) copy-start(f32[64]{0:T(128)} %param.19) | copy-start | bytes 772
  22.0 24.9 %copy-start.3 = (f32[1,128,256]{2,1,0:T(8,128)S(1)}, f32[1,128,256]{2,1,0:T(8,128)}, u32[]{:S(2)}) copy-start(f32[1,128,256]{2,1,0:T(8,128)} %param.14) | copy-start | bytes 393220
  35.5 25.4 %copy-start.4 = (f32[64,512]{1,0:T(8,128)S(1)}, f32[64,512]{1,0:T(8,128)}, u32[]{:S(2)}) copy-start(f32[64,512]{1,0:T(8,128)} %param.17) | copy-start | bytes 393220
  35.5 11.3 %all-to-all-start = ((f32[2,1,128,256]{3,2,1,0:T(8,128)}), f32[2,1,128,256]{3,2,1,0:T(8,128)S(1)}, u32[]{:S(2)}, u32[]{:S(2)}) async-start(f32[2,1,128,256]{3,2,1,0:T(8,128)} %fusion.2), calls=%async_computation | async-start | bytes 524288 | tf_op jit(solution)/shard_map/all_to_all | solution.py:20
  53.4 14.8 %all-to-all-start.2 = ((f32[32,2,1,2,256]{4,1,3,2,0:T(2,128)}), f32[32,2,1,2,256]{4,1,3,2,0:T(2,128)S(1)}, u32[]{:S(2)}, u32[]{:S(2)}) async-start(f32[32,2,1,2,256]{4,1,3,2,0:T(2,128)} %copy.42), calls=%async_computation.2 | async-start | bytes 262144 | tf_op jit(solution)/shard_map/all_to_all | solution.py:34
  72.2 14.1 %all-to-all-start.3 = ((bf16[64,2,256]{2,1,0:T(2,128)(2,1)}), bf16[64,2,256]{2,1,0:T(2,128)(2,1)S(1)}, u32[]{:S(2)}, u32[]{:S(2)}) async-start(bf16[64,2,256]{2,1,0:T(2,128)(2,1)} %copy.46), calls=%async_computation.3 | async-start | bytes 131072 | tf_op jit(solution)/shard_map/all_to_all | solution.py:124
  87.1 8.2 %all-to-all-start.4 = ((bf16[2,1,128,256]{2,3,1,0:T(8,128)(2,1)}), bf16[2,1,128,256]{2,3,1,0:T(8,128)(2,1)S(1)}, u32[]{:S(2)}, u32[]{:S(2)}) async-start(bf16[2,1,128,256]{2,3,1,0:T(8,128)(2,1)} %broadcast_in_dim.54), calls=%async_computation.4 | async-start | bytes 262144 | tf_op jit(solution)/shard_map/all_to_all | solution.py:46
  116.0 6.6 %collective-permute-start = (bf16[1,128,512]{1,2,0:T(8,128)(2,1)S(1)}, bf16[1,128,512]{1,2,0:T(8,128)(2,1)S(1)}, u32[]{:S(2)}, u32[]{:S(2)}) collective-permute-start(bf16[1,128,512]{1,2,0:T(8,128)(2,1)S(1)} %bitcast_select_fusion), channel_id=1, source_target_pairs={{0,126},{2,0},{4,2},{6,4},{8,6},{10,8},{12,10},{14,12},{16,14},{18... | collective-permute-start | bytes 393224 | tf_op jit(solution)/shard_map/ppermute | solution.py:58
  121.8 7.7 %collective-permute-start.1 = (bf16[1,128,512]{1,2,0:T(8,128)(2,1)S(1)}, bf16[1,128,512]{1,2,0:T(8,128)(2,1)S(1)}, u32[]{:S(2)}, u32[]{:S(2)}) collective-permute-start(bf16[1,128,512]{1,2,0:T(8,128)(2,1)S(1)} %bitcast_select_fusion.1), channel_id=1, source_target_pairs={{0,2},{2,4},{4,6},{6,8},{8,10},{10,12},{12,14},{14,16},{16,18},{18... | collective-permute-start | bytes 393224 | tf_op jit(solution)/shard_map/ppermute | solution.py:58
where the time goes:
time: 144 us; the launch traced here: 143 us
  local copies, waits for them, and re-layouts  48.9 us (34%)
  matrix products  27.1 us (19%)
  starting transfers between devices  24.8 us (17%)
  waiting for transfers between devices  19.8 us (14%)
  other arithmetic  14.8 us (10%)
  blocking collectives  5.59 us (4%)
  between operations  1.64 us (1%)
    dot_general x1, local copies, waits for them, and re-layouts, shards(): jnp.dot(loads.reshape(local_sec * rows_two, dof_rows), modes, preferred_e...  21.3 us
    scatter x2, other arithmetic, shards(): raw.at[:, :, iface_right].set(right_new).at[:, :, iface_left].set(left_new)  13.7 us
    dot_general x1, matrix products, shards(): jnp.dot(loads.reshape(local_sec * rows_two, dof_rows), modes, preferred_e...  13.5 us
    dot_general x1, matrix products, shards(): jnp.einsum('skm,dm->skd', gather_directly(rounded, 'dof', 2), modes, pref...  10.4 us
    all_to_all x1, waiting for transfers between devices, shards(): lax.all_to_all(jnp.stack([out_re, out_im], 1).astype(jnp.bfloat16), SECTO...  8.13 us
    all_to_all x1, starting transfers between devices, exchange_in_order(): result = lax.all_to_all(result, axes[k], k, k, tiled=True)  7.5 us
    unnamed x16, local copies, waits for them, and re-layouts  6.51 us
    convert_element_type x1, local copies, waits for them, and re-layouts, shards(): raw = jnp.einsum('skm,dm->skd', gather_directly(rounded, 'dof', 2), modes...  6.37 us
  transfers between devices with their start and end apart: 6, of which 4 were waited for; matrix products, arithmetic and copies ran while one was open for 12% of the time, Pallas kernels for 0%

commit v1 on v0

v1 whole, which is shorter than its diff:
```python
import functools
import math

import jax
import jax.numpy as jnp
import numpy as np
from jax import lax
from jax.experimental import pallas as pl
from jax.experimental.pallas import tpu as pltpu
from jax.sharding import Mesh
from jax.sharding import PartitionSpec as P

SECTOR = ("sector_0", "sector_1", "sector_2", "sector_3")
EVERY = SECTOR + ("dof",)
BF16 = jnp.bfloat16
F32 = jnp.float32
EMPTY = 3.0e38


def one_hot_rows(target):
    out = np.zeros((len(target), int(max(target)) + 1 if len(target) else 0), np.float32)
    out[np.arange(len(target)), target] = 1.0
    return out


def split_bf16(table):
    high = table.astype(np.float32).astype(jnp.bfloat16)
    low = (table - high.astype(np.float64)).astype(np.float32).astype(jnp.bfloat16)
    return high, low


def constants(sectors, dofs, freqs):
    turns = np.outer(np.arange(sectors), np.arange(sectors)) % sectors
    theta = turns * (2.0 * math.pi / sectors)
    cosine, sine = np.cos(theta), np.sin(theta)
    forward = np.zeros((2, sectors, sectors, dofs, 2))
    for d in range(dofs):
        forward[0, :, :, d, 0] = cosine
        forward[0, :, :, d, 1] = sine
        forward[1, :, :, d, 0] = -sine
        forward[1, :, :, d, 1] = cosine
    forward = forward.reshape(2 * sectors, sectors * dofs * 2)
    inverse = np.zeros((sectors, 2, 2, sectors))
    inverse[:, 0, 0, :] = cosine / sectors
    inverse[:, 0, 1, :] = -sine / sectors
    inverse[:, 1, 0, :] = sine / sectors
    inverse[:, 1, 1, :] = cosine / sectors
    inverse = inverse.reshape(2 * sectors, 2 * sectors)
    return split_bf16(forward), split_bf16(inverse)


def dot(a, b):
    return jnp.dot(a, b, preferred_element_type=F32)


def dot_t(a, b):
    return lax.dot_general(a, b, (((1,), (1,)), ((), ())), preferred_element_type=F32)


def one_hot(rows, cols, target):
    at = lax.broadcasted_iota(jnp.int32, (rows, cols), 1)
    row = lax.broadcasted_iota(jnp.int32, (rows, cols), 0)
    return jnp.where(target(row) == at, 1.0, 0.0).astype(BF16)


def force_kernel(steps, pattern, loads, modes, response, deviation, out, total):
    step = pl.program_id(0)

    @pl.when(step == 0)
    def _():
        total[...] = jnp.zeros_like(total)

    total[...] += dot(loads[...], modes[...])

    @pl.when(step == steps - 1)
    def _():
        half = response.shape[1]
        mine = pl.ds(pl.multiple_of(lax.axis_index("dof") * half, half), half)
        row = deviation[pl.ds(pattern[0], 1), mine]
        total[:, mine] -= row * response[...]
        rows = total.shape[0]
        freqs = rows // 2
        stacked = jnp.concatenate([total[:, :half], total[:, half:]], 0).astype(BF16)

        def source(row):
            return (row // 2 % 2) * rows + (row % 2) * freqs + row // 4

        order = one_hot(2 * rows, 2 * rows, source)
        out[...] = dot(order, stacked).astype(BF16)


def force(loads, modes, response, pattern, deviation):
    rows, depth = loads.shape
    width = modes.shape[1]
    half = response.shape[1]
    block = 2048
    steps = depth // block
    return pl.pallas_call(
        functools.partial(force_kernel, steps),
        grid=(steps,),
        out_shape=jax.ShapeDtypeStruct((2 * rows, half), BF16),
        in_specs=[
            pl.BlockSpec(memory_space=pltpu.SMEM),
            pl.BlockSpec((rows, block), lambda k: (0, k)),
            pl.BlockSpec((block, width), lambda k: (k, 0)),
            pl.BlockSpec((rows, half), lambda k: (0, 0)),
            pl.BlockSpec(deviation.shape, lambda k: (0, 0)),
        ],
        out_specs=pl.BlockSpec((2 * rows, half), lambda k: (0, 0)),
        scratch_shapes=[pltpu.VMEM((rows, width), F32)],
        compiler_params=pltpu.CompilerParams(
            dimension_semantics=("arbitrary",), vmem_limit_bytes=24 << 20
        ),
        cost_estimate=pl.CostEstimate(
            flops=2 * rows * depth * width, bytes_accessed=2 * depth * (rows + width), transcendentals=0
        ),
        name="force",
    )(pattern, loads, modes, response, deviation)


def split_here(value):
    high = value.astype(BF16)
    return high, (value - high.astype(F32)).astype(BF16)


def solve_kernel(omega_sq, got, fwd_hi, fwd_lo, inv_hi, inv_lo, eigen, loss, out):
    sectors = eigen.shape[0]
    half = got.shape[1]
    me = lax.axis_index(EVERY)
    side, freq = me % 2, me // 2
    spec = dot(fwd_hi[...], got[...]) + dot(fwd_lo[...], got[...])
    p, q = spec[:sectors], spec[sectors:]
    mine = pl.ds(pl.multiple_of(side * half, half), half)
    stiff = eigen[:, mine]
    a = stiff - omega_sq[freq]
    b = loss[:, mine] * stiff
    denom = a * a + b * b
    solved = jnp.concatenate([(p * a + q * b) / denom, (q * a - p * b) / denom], 0)
    high, low = split_here(solved)
    result = dot(inv_hi[...], high) + (dot(inv_hi[...], low) + dot(inv_lo[...], high))
    result = result.astype(BF16)

    def source(row):
        sector, place = row // 16, row % 8
        near = (sector + place // 2 + sectors - 1) % sectors
        return jnp.where(place < 6, near * 2 + place % 2, -1)

    order = one_hot(out.shape[0], 2 * sectors, source)
    out[...] = dot(order, result).astype(BF16)


def solve(got, fwd, inv, eigen, loss, omega_sq):
    sectors = eigen.shape[0]
    half = got.shape[1]
    whole = lambda s: pl.BlockSpec(memory_space=pltpu.VMEM)
    args = (got, *fwd, *inv, eigen, loss)
    return pl.pallas_call(
        solve_kernel,
        out_shape=jax.ShapeDtypeStruct((sectors * 16, half), BF16),
        in_specs=[pl.BlockSpec(memory_space=pltpu.SMEM)] + [whole(a) for a in args],
        out_specs=pl.BlockSpec(memory_space=pltpu.VMEM),
        compiler_params=pltpu.CompilerParams(vmem_limit_bytes=24 << 20),
        name="solve",
    )(omega_sq, *args)


def recover_kernel(
    tiles, index, got, near, modes, modal, shown, resp, spread, fresh
):
    step = pl.program_id(0)
    rows, width = resp.shape[1:]
    half = got.shape[1]
    freqs = rows // 2
    tile = modes.shape[0]
    entries = near.shape[0]

    @pl.when(step == 0)
    def _():
        per = 256 // 16

        def source(row):
            side, place, f = row // (6 * per), row // per % 6, row % per
            return f * 16 + side * 8 + place

        order = one_hot(12 * per, 256, source)
        for t in range(freqs // per):
            part = dot(order, got[256 * t : 256 * (t + 1), :]).astype(BF16)
            for side in range(2):
                for place in range(6):
                    at = (side * 6 + place) * per
                    resp[
                        place // 2,
                        (place % 2) * freqs + t * per : (place % 2) * freqs + (t + 1) * per,
                        side * half : (side + 1) * half,
                    ] = part[at : at + per]
        mine = pl.ds(pl.multiple_of(lax.axis_index("dof") * half, half), half)
        modal[...] = resp[1, :, mine].astype(F32)

        count = entries // 2
        left, right = near[:count, :], near[count:, :]
        rounded = lambda a, b: dot_t(a, b).astype(BF16).astype(F32)
        fresh[:count, :] = 0.5 * (rounded(right, resp[0]) + rounded(left, resp[1]))
        fresh[count:, :] = 0.5 * (rounded(right, resp[1]) + rounded(left, resp[2]))

        spread[...] = jnp.full(spread.shape, EMPTY, F32)

        def put(i, carry):
            for j in range(8):
                at = i * 8 + j
                spread[pl.ds(index[at], 1), :] = fresh[pl.ds(at, 1), :]
            return carry

        lax.fori_loop(0, entries // 8, put, 0)

    raw = dot_t(resp[1], modes[...]).astype(BF16)
    here = spread[pl.ds(pl.multiple_of(step * tile, tile), tile), :].astype(BF16).T
    shown[...] = jnp.where(here < 1e38, here, raw)


def recover(got, near, modes, index, rows, half):
    depth, width = modes.shape
    tile = 1024
    tiles = depth // tile
    entries = near.shape[0]
    return pl.pallas_call(
        functools.partial(recover_kernel, tiles),
        grid=(tiles,),
        out_shape=(
            jax.ShapeDtypeStruct((rows, half), F32),
            jax.ShapeDtypeStruct((rows, depth), BF16),
        ),
        in_specs=[
            pl.BlockSpec(memory_space=pltpu.SMEM),
            pl.BlockSpec(got.shape, lambda k: (0, 0)),
            pl.BlockSpec(near.shape, lambda k: (0, 0)),
            pl.BlockSpec((tile, width), lambda k: (k, 0)),
        ],
        out_specs=(
            pl.BlockSpec((rows, half), lambda k: (0, 0)),
            pl.BlockSpec((rows, tile), lambda k: (0, k)),
        ),
        scratch_shapes=[
            pltpu.VMEM((3, rows, width), BF16),
            pltpu.VMEM((depth, rows), F32),
            pltpu.VMEM((entries, rows), F32),
        ],
        compiler_params=pltpu.CompilerParams(
            dimension_semantics=("arbitrary",), vmem_limit_bytes=32 << 20
        ),
        name="recover",
    )(index, got, near, modes)


def exchange(pieces):
    return lax.all_to_all(pieces, EVERY, 0, 0, tiled=True)


def shards(
    loads, modes, response, pattern, deviation, eigen, loss, omega_sq, iface_left, iface_right
):
    rows = loads.shape[1]
    half = response.shape[2]
    devices = lax.axis_size(EVERY)
    sectors = lax.axis_size(SECTOR)
    dofs = lax.axis_size("dof")
    fwd, inv = constants(sectors, dofs, rows // 2)
    sent = force(loads[0], modes, response[0], pattern, deviation)
    got = exchange(sent.reshape(devices, -1, half)).reshape(-1, half)
    back = solve(got, fwd, inv, eigen, loss[None], omega_sq)
    index = jnp.concatenate([iface_left, iface_right])
    near = jnp.take(modes, index, axis=0, mode="clip")
    seen = exchange(back.reshape(devices, -1, half)).reshape(-1, half)
    modal, shown = recover(seen, near, modes, index, rows, half)
    return modal[None], shown[None]


def solution(mesh):
    torus = Mesh(
        mesh.devices.reshape(4, 4, 2, 2, mesh.shape["dof"]),
        ("sector_0", "sector_1", "sector_2", "sector_3", "dof"),
    )
    return jax.shard_map(
        shards,
        mesh=torus,
        in_specs=(
            P(SECTOR, None, "dof"),
            P("dof", None),
            P(SECTOR, None, "dof"),
            P(SECTOR),
            P(),
            P(),
            P(),
            P(),
            P("dof"),
            P("dof"),
        ),
        out_specs=(P(SECTOR, None, "dof"), P(SECTOR, None, "dof")),
        check_vma=False,
    )
```

time: 144 us -> 76.5 us (0.53)
  matrix products: 27.1 us -> 0 us
  local copies, waits for them, and re-layouts: 48.9 us -> 27.4 us
  starting transfers between devices: 24.8 us -> 4.11 us
  Pallas kernels: 0 us -> 20 us
  waiting for transfers between devices: 19.8 us -> 1.7 us
  blocking collectives: 5.59 us -> 21.4 us
  other arithmetic: 14.8 us -> 0.01 us
    dot_general x11 -> x0, matrix products: 27.1 us -> none  [the longest x1 13.5 us: shards(): jnp.dot(loads.reshape(local_sec * rows_two, dof_rows), modes, preferred_e...]
    dot_general x1 -> x0, local copies, waits for them, and re-layouts: 21.3 us -> none  [shards(): jnp.dot(loads.reshape(local_sec * rows_two, dof_rows), modes, preferred_e...]
    pallas_call x0 -> x3, Pallas kernels: none -> 20 us  [the longest x1 13.4 us: recover(): pl.pallas_call(functools.partial(recover_kernel, tiles), grid=(tiles,), o...]
    all_to_all x4 -> x1, starting transfers between devices: 22.8 us -> 4.11 us  [exchange(): return lax.all_to_all(pieces, EVERY, 0, 0, tiled=True)]
    all_to_all x4 -> x1, waiting for transfers between devices: 19.8 us -> 1.7 us  [exchange(): return lax.all_to_all(pieces, EVERY, 0, 0, tiled=True)]
    all_to_all x1, blocking collectives: 5.59 us -> 21.4 us  [exchange(): return lax.all_to_all(pieces, EVERY, 0, 0, tiled=True)]
    scatter x2 -> x0, other arithmetic: 13.7 us -> none  [shards(): raw.at[:, :, iface_right].set(right_new).at[:, :, iface_left].set(left_new)]
    unnamed x16 -> x29, local copies, waits for them, and re-layouts: 6.51 us -> 15.4 us
  transfers between devices with their start and end apart: 6 -> 1, of which waited for: 4 -> 1; matrix products, arithmetic and copies ran while one was open for 12% -> 16% of each run, Pallas kernels for 0% -> 0%
where the time goes in v1:
time: 76.5 us; the launch traced here: 76.1 us
  local copies, waits for them, and re-layouts  27.4 us (36%)
  blocking collectives  21.4 us (28%)
  Pallas kernels  20 us (26%)
  starting transfers between devices  4.11 us (5%)
  waiting for transfers between devices  1.7 us (2%)
  between operations  1.5 us (2%)
    all_to_all x1, blocking collectives, exchange(): return lax.all_to_all(pieces, EVERY, 0, 0, tiled=True)  21.4 us
    unnamed x29, local copies, waits for them, and re-layouts  15.4 us
    pallas_call x1, Pallas kernels, recover(): pl.pallas_call(functools.partial(recover_kernel, tiles), grid=(tiles,), o...  13.4 us
    gather x1, local copies, waits for them, and re-layouts, shards(): near = jnp.take(modes, index, axis=0, mode='clip')  11.9 us
    pallas_call x1, Pallas kernels, force(): pl.pallas_call(functools.partial(force_kernel, steps), grid=(steps,), out...  4.25 us
    all_to_all x1, starting transfers between devices, exchange(): return lax.all_to_all(pieces, EVERY, 0, 0, tiled=True)  4.11 us
    pallas_call x1, Pallas kernels, solve(): pl.pallas_call(solve_kernel, out_shape=jax.ShapeDtypeStruct((sectors * 16...  2.36 us
    all_to_all x1, waiting for transfers between devices, exchange(): return lax.all_to_all(pieces, EVERY, 0, 0, tiled=True)  1.7 us
  transfers between devices with their start and end apart: 1, of which 1 were waited for; matrix products, arithmetic and copies ran while one was open for 16% of the time, Pallas kernels for 0%

profile of v1, /device:TPU:1, one launch (start us, length us, event | category | flops | bytes accessed | tf_op | source)
XLA Modules:
  0.0 76.1 jit_solution(14418863228500266331)
XLA Ops:
  0.6 0.0 copy-start.11
  0.6 0.0 copy-start.10
  0.7 0.0 copy-start.12
  1.3 0.0 copy-start
  1.3 5.8 %copy-done = bf16[16384,512]{1,0:T(8,128)(2,1)S(1)} copy-done((bf16[16384,512]{1,0:T(8,128)(2,1)S(1)}, bf16[16384,512]{1,0:T(8,128)(2,1)}, u32[]{:S(2)}) %copy-start) | copy-done | bytes 16777240
  7.1 2.2 %copy-done.2 = bf16[1,128,16384]{2,1,0:T(8,128)(2,1)S(1)} copy-done((bf16[1,128,16384]{2,1,0:T(8,128)(2,1)S(1)}, bf16[1,128,16384]{2,1,0:T(8,128)(2,1)}, u32[]{:S(2)}) %copy-start.2) | copy-done | bytes 4194328
  9.3 0.9 %copy-done.3 = f32[1,128,256]{2,1,0:T(8,128)S(1)} copy-done((f32[1,128,256]{2,1,0:T(8,128)S(1)}, f32[1,128,256]{2,1,0:T(8,128)}, u32[]{:S(2)}) %copy-start.3) | copy-done | bytes 131096
  10.2 0.7 copy-done.9
  10.9 0.0 copy-start.8
  10.9 0.0 copy-start.13
  11.0 4.2 %force.1 = bf16[256,256]{1,0:T(8,128)(2,1)S(1)} custom-call(s32[1]{0:T(128)S(6)} %copy.18.pattern, bf16[128,16384]{1,0:T(8,128)(2,1)S(1)} %bitcast.7, bf16[16384,512]{1,0:T(8,128)(2,1)S(1)} %copy-done, f32[128,256]{1,0:T(8,128)S(1)} %bitcast.9, f32[8,512]{1,0:T(8,128)S(1)} %copy-done.9), custom_call_target="tpu_custom_call" | custom-call | flops 2147483648 | bytes 20971520 | tf_op jit(solution)/shard_map/force/pallas_call | solution.py:98
  15.2 0.1 reshape.16
  15.3 21.4 %all_to_all.10 = bf16[128,2,256]{2,1,0:T(2,128)(2,1)S(1)} all-to-all(bf16[128,2,256]{2,1,0:T(2,128)(2,1)S(1)} %reshape.16), channel_id=1, replica_groups=mesh['sector_0'=4,'sector_1'=4,'sector_2'=2,'sector_3'=2,'dof'=2] {'sect..., dimensions={0} | all-to-all | bytes 262144 | tf_op jit(solution)/shard_map/all_to_all | solution.py:255
  36.7 0.1 reshape.17.got
  36.8 0.0 copy-done.11
  36.8 0.0 copy-done.10
  36.8 0.0 copy-done.4
  36.8 0.0 copy-done.5
  36.8 2.4 %solve.1 = bf16[1024,256]{1,0:T(8,128)(2,1)} custom-call(f32[64]{0:T(128)S(1)} %copy-done.11, bf16[256,256]{1,0:T(8,128)(2,1)S(1)} %reshape.17.got, bf16[128,256]{1,0:T(8,128)(2,1)S(1)} %copy-done.6, bf16[128,256]{1,0:T(8,128)(2,1)S(1)} %copy-done.5, bf16[128,128]{1,0:T(8,128)(2,1)S(1)} %copy-done.8, bf16[128,128]{1,0:T(8,128)(2,1)S(1)} %copy-done.7, ...), custom_call_target="tpu_custom_call" | custom-call | tf_op jit(solution)/shard_map/solve/pallas_call | solution.py:157
  39.2 4.1 %all-to-all-start.1 = ((bf16[128,8,256]{2,1,0:T(8,128)(2,1)}), bf16[128,8,256]{2,1,0:T(8,128)(2,1)S(1)}, u32[]{:S(2)}, u32[]{:S(2)}) async-start(bf16[128,8,256]{2,1,0:T(8,128)(2,1)} %bitcast.3), calls=%async_computation.1 | async-start | bytes 1048576 | tf_op jit(solution)/shard_map/all_to_all | solution.py:255
  43.4 11.9 %gather_fusion = bf16[1024,512]{1,0:T(8,128)(2,1)S(1)} fusion(bf16[16384,512]{1,0:T(8,128)(2,1)} %modes.3, s32[1024]{0:T(1024)S(1)} %broadcast_clamp_fusion), kind=kCustom, calls=%fused_computation | custom fusion | bytes 2101248 | tf_op jit(solution)/shard_map/jit(_take)/gather | solution.py:271
  55.3 1.7 %all-to-all-done.1 = bf16[128,8,256]{2,1,0:T(8,128)(2,1)S(1)} async-done(((bf16[128,8,256]{2,1,0:T(8,128)(2,1)}), bf16[128,8,256]{2,1,0:T(8,128)(2,1)S(1)}, u32[]{:S(2)}, u32[]{:S(2)}) %all-to-all-start.1) | async-done | bytes 524320 | tf_op jit(solution)/shard_map/all_to_all | solution.py:255
  57.0 5.8 %copy-done.1 = bf16[16384,512]{1,0:T(8,128)(2,1)S(1)} copy-done((bf16[16384,512]{1,0:T(8,128)(2,1)S(1)}, bf16[16384,512]{1,0:T(8,128)(2,1)}, u32[]{:S(2)}) %copy-start.1) | copy-done | bytes 16777240
  62.8 13.4 %recover.1 = (f32[128,256]{1,0:T(8,128)}, bf16[128,16384]{1,0:T(8,128)(2,1)}) custom-call(s32[1024]{0:T(1024)S(1)} %constant_dynamic-update-slice_fusion.index, bf16[1024,256]{1,0:T(8,128)(2,1)S(1)} %bitcast.8, bf16[1024,512]{1,0:T(8,128)(2,1)S(1)} %gather_fusion, bf16[16384,512]{1,0:T(8,128)(2,1)S(1)} %copy-done.1), custom_call_target="tpu_custom_call" | custom-call | tf_op jit(solution)/shard_map/recover/pallas_call | solution.py:225
  (17 shorter events, 0.0 us)
Async XLA Ops:
  0.6 36.1 %copy-start.11 = (f32[64]{0:T(128)S(1)}, f32[64]{0:T(128)}, u32[]{:S(2)}) copy-start(f32[64]{0:T(128)} %omega_sq.1) | copy-start | bytes 772
  0.6 36.1 %copy-start.10 = (f32[512]{0:T(512)S(1)}, f32[512]{0:T(512)}, u32[]{:S(2)}) copy-start(f32[512]{0:T(512)} %param.20) | copy-start | bytes 6148
  0.7 42.7 %copy-start.12 = (s32[512]{0:T(512)S(1)}, s32[512]{0:T(512)}, u32[]{:S(2)}) copy-start(s32[512]{0:T(512)} %param.22) | copy-start | bytes 6148
  1.3 5.8 %copy-start = (bf16[16384,512]{1,0:T(8,128)(2,1)S(1)}, bf16[16384,512]{1,0:T(8,128)(2,1)}, u32[]{:S(2)}) copy-start(bf16[16384,512]{1,0:T(8,128)(2,1)} %modes.3) | copy-start | bytes 50331652
  7.1 2.2 %copy-start.2 = (bf16[1,128,16384]{2,1,0:T(8,128)(2,1)S(1)}, bf16[1,128,16384]{2,1,0:T(8,128)(2,1)}, u32[]{:S(2)}) copy-start(bf16[1,128,16384]{2,1,0:T(8,128)(2,1)} %param.14) | copy-start | bytes 12582916
  9.3 0.9 %copy-start.3 = (f32[1,128,256]{2,1,0:T(8,128)S(1)}, f32[1,128,256]{2,1,0:T(8,128)}, u32[]{:S(2)}) copy-start(f32[1,128,256]{2,1,0:T(8,128)} %param.16) | copy-start | bytes 393220
  10.2 0.7 copy-start.9
  10.9 25.9 %copy-start.4 = (f32[64,512]{1,0:T(8,128)S(1)}, f32[64,512]{1,0:T(8,128)}, u32[]{:S(2)}) copy-start(f32[64,512]{1,0:T(8,128)} %eigen.1) | copy-start | bytes 393220
  10.9 25.9 %copy-start.5 = (bf16[128,256]{1,0:T(8,128)(2,1)S(1)}, bf16[128,256]{1,0:T(8,128)(2,1)}, u32[]{:S(2)}) copy-start(bf16[128,256]{1,0:T(8,128)(2,1)} %constant.9.clone.fwd_lo) | copy-start | bytes 196612
  10.9 25.9 %copy-start.6 = (bf16[128,256]{1,0:T(8,128)(2,1)S(1)}, bf16[128,256]{1,0:T(8,128)(2,1)}, u32[]{:S(2)}) copy-start(bf16[128,256]{1,0:T(8,128)(2,1)} %constant.8.clone.fwd_hi) | copy-start | bytes 196612
  10.9 25.9 %copy-start.7 = (bf16[128,128]{1,0:T(8,128)(2,1)S(1)}, bf16[128,128]{1,0:T(8,128)(2,1)}, u32[]{:S(2)}) copy-start(bf16[128,128]{1,0:T(8,128)(2,1)} %constant.11.clone.inv_lo) | copy-start | bytes 98308
  10.9 25.9 %copy-start.8 = (bf16[128,128]{1,0:T(8,128)(2,1)S(1)}, bf16[128,128]{1,0:T(8,128)(2,1)}, u32[]{:S(2)}) copy-start(bf16[128,128]{1,0:T(8,128)(2,1)} %constant.10.clone.inv_hi) | copy-start | bytes 98308
  10.9 32.4 %copy-start.13 = (s32[512]{0:T(512)S(1)}, s32[512]{0:T(512)}, u32[]{:S(2)}) copy-start(s32[512]{0:T(512)} %param.23) | copy-start | bytes 6148
  39.2 17.8 %all-to-all-start.1 = ((bf16[128,8,256]{2,1,0:T(8,128)(2,1)}), bf16[128,8,256]{2,1,0:T(8,128)(2,1)S(1)}, u32[]{:S(2)}, u32[]{:S(2)}) async-start(bf16[128,8,256]{2,1,0:T(8,128)(2,1)} %bitcast.3), calls=%async_computation.1 | async-start | bytes 1048576 | tf_op jit(solution)/shard_map/all_to_all | solution.py:255
  57.0 5.8 %copy-start.1 = (bf16[16384,512]{1,0:T(8,128)(2,1)S(1)}, bf16[16384,512]{1,0:T(8,128)(2,1)}, u32[]{:S(2)}) copy-start(bf16[16384,512]{1,0:T(8,128)(2,1)} %modes.3) | copy-start | bytes 50331652
